TPU v7x, 32 devices: a whole 2x2x4 slice. The times are simulated.
32 devices in a mesh: rows: 8 (over z, x), cols: 4 (over y, core).
Axes of the slice: x: 2, y: 2, z: 4, core: 2. Of those that a mesh axis runs over, the one named last changes fastest.
Arguments:
- rhs: float32 [2, 4096, 512], P(None, 'rows', 'cols'), may hold values from -6 to 6
- diag_blocks: float32 [2, 512, 512], replicated, may hold values from -0.25 to 0.25
- multipliers: float32 [2, 2, 4096, 512], P(None, None, 'rows'), may hold values from -0.25 to 0.25
- pivots: int32 [1024], P('cols'), may hold values from 0 to 8191, as said below
Outputs:
- solved: float32 [2, 4096, 512], P(None, 'rows', 'cols')
Inputs may be any that keep to these rules, and one draw needn't show every extreme that they name: pivots[i] is i or a row at 1024 or beyond; the rows at 1024 or beyond that pivots names are all different, and at most 192 of them lie among the rows held by one index of rows, a number that some index reaches.
All inputs are finite; a program needn't handle non-finite values.
Results may differ from a plain program's by a relative error of at most 0.0001.
Values sent between devices are 32-bit elements; how exact they have to be, the bound alone decides.
A program may use at most 64 MiB of HBM per device.

v0:
```python
import jax
import jax.numpy as jnp
from jax import lax
from jax.sharding import PartitionSpec as P


def broadcast(block, axis, holder):
    block = jnp.where(lax.axis_index(axis) == holder, block, jnp.zeros_like(block))
    return lax.psum(block, axis)


def unit_lower_solve(factor, values):
    return lax.linalg.triangular_solve(
        factor, values, left_side=True, lower=True, unit_diagonal=True
    )


def product(left, right):
    return jnp.dot(left, right, precision=lax.Precision.HIGHEST, preferred_element_type=jnp.float32)


def shards(rhs, diag_blocks, multipliers, pivots):
    cycles, blk, columns = rhs.shape
    ranks = lax.axis_size("rows")
    mine = lax.axis_index("rows")
    stride = ranks * blk
    local_count = cycles * blk
    listed = lax.all_gather(pivots, "cols", axis=0, tiled=True)
    count = listed.shape[0]
    places = jnp.arange(count, dtype=jnp.int32)
    fresh = listed >= count
    fresh_targets = jnp.where(fresh, listed, 0)
    flat = rhs.reshape(local_count, columns)

    def locate(global_row):
        inner = global_row % stride
        return (global_row // stride, inner // blk, inner % blk)

    def fetch(source_rows):
        src_cycle, src_owner, src_row = locate(source_rows)
        return (jnp.take(flat, src_cycle * blk + src_row, axis=0), src_owner)

    def landing_of(global_rows, keep):
        dst_cycle, dst_owner, dst_row = locate(global_rows)
        return jnp.where(keep & (dst_owner == mine), dst_cycle * blk + dst_row, local_count)

    panel_here, panel_src = fetch(listed)
    panel_contrib = jnp.where((panel_src == mine)[:, None], panel_here, 0.0)
    fresh_here, fresh_src = fetch(places)
    panel_landing = landing_of(places, places < count)
    fresh_landing = landing_of(fresh_targets, fresh)
    fresh_contrib = jnp.where((fresh & (fresh_src == mine))[:, None], fresh_here, 0.0)
    moved = lax.psum(jnp.concatenate([panel_contrib, fresh_contrib], axis=0), "rows")
    panel_moved = moved[:count]
    fresh_moved = moved[count:]
    permuted = (
        flat.at[panel_landing]
        .set(panel_moved, mode="drop")
        .at[fresh_landing]
        .set(fresh_moved, mode="drop")
    )
    lower = multipliers.reshape(multipliers.shape[0], local_count, blk)
    first_block = unit_lower_solve(diag_blocks[0], panel_moved[:blk])
    below = broadcast(lower[0, :blk], "rows", 1)
    started = panel_moved[blk : 2 * blk] - product(below, first_block)
    second_block = unit_lower_solve(diag_blocks[1], started)
    local_rows = jnp.arange(local_count, dtype=jnp.int32)
    global_rows = local_rows // blk * stride + mine * blk + local_rows % blk
    result = permuted
    result = jnp.where(
        (global_rows >= blk)[:, None], result - product(lower[0], first_block), result
    )
    result = jnp.where(
        (global_rows >= 2 * blk)[:, None], result - product(lower[1], second_block), result
    )
    padding = jnp.zeros(((cycles - 1) * blk, columns), jnp.float32)
    head_first = jnp.concatenate([first_block, padding], axis=0)
    head_second = jnp.concatenate([second_block, padding], axis=0)
    result = jnp.where((global_rows < blk)[:, None], head_first, result)
    result = jnp.where(
        ((global_rows >= blk) & (global_rows < 2 * blk))[:, None], head_second, result
    )
    return result.reshape(cycles, blk, columns)


def solution(mesh):
    placed = (P(None, "rows", "cols"), P(), P(None, None, "rows", None), P("cols"))
    return jax.shard_map(
        shards, mesh=mesh, in_specs=placed, out_specs=P(None, "rows", "cols"), check_vma=False
    )
```

profile of v0, /device:TPU:0, one launch (start us, length us, event | category | flops | bytes accessed | tf_op | source)
XLA Modules:
  0.0 159.9 jit_solution(16290753989849099606)
XLA Ops:
  6.5 1.0 copy.32
  7.6 6.3 %all-gather = s32[4,1,256]{2,1,0:T(1,128)S(1)} all-gather(s32[1,1,256]{2,1,0:T(1,128)} %bitcast.99), channel_id=1, replica_groups=mesh['rows'=8,'cols'=4] {'cols'}, dimensions={0}, use_global_device_ids=true | all-gather | bytes 5120 | tf_op jit(solution)/shard_map/all_gather | solution.py:28
  14.0 2.8 %gather_fusion = f32[1024,128]{1,0:T(8,128)S(1)} fusion(f32[1024,128]{1,0:T(8,128)S(1)} %bitcast.90, s32[1024]{0:T(1024)S(1)} %broadcast_clamp_fusion.1), kind=kCustom, calls=%fused_computation.clone | custom fusion | bytes 1052672 | tf_op jit(solution)/shard_map/jit(_take)/gather | solution.py:41
  16.8 2.8 %gather_fusion.1 = f32[1024,128]{1,0:T(8,128)S(1)} fusion(f32[1024,128]{1,0:T(8,128)S(1)} %bitcast.91, s32[1024]{0:T(1024)S(1)} %broadcast_clamp_fusion), kind=kCustom, calls=%fused_computation.1.clone | custom fusion | bytes 1052672 | tf_op jit(solution)/shard_map/jit(_take)/gather | solution.py:41
  21.6 2.3 %fusion.6 = f32[512,512]{1,0:T(8,128)} fusion(f32[2,1024,512]{2,1,0:T(8,128)} %bitcast.95, pred[]{:T(512)S(6)} %eq.43), kind=kLoop, calls=%fused_computation.26 | loop fusion | flops 262144 | bytes 2097153 | tf_op jit(solution)/shard_map/jit(_where)/select_n | solution.py:8
  23.9 1.7 %convert_add_fusion.1 = (f32[512,512]{1,0:T(8,128)S(1)}, f32[512,512]{1,0:T(8,128)S(1)}) fusion(f32[2,512,512]{2,1,0:T(8,128)} %param.9, s32[512]{0:T(512)S(1)} %iota_add_fusion), kind=kLoop, calls=%fused_computation.9 | loop fusion | flops 1835008 | bytes 4196352 | tf_op jit(solution)/shard_map/triangular_solve/add.1 | solution.py:13
  25.7 7.7 %while.4 = (s32[]{:T(128)}, f32[512,512]{1,0:T(8,128)S(1)}, s32[4,2]{0,1:T(2,128)S(1)}, f32[4,128,128]{2,1,0:T(8,128)S(1)}, s32[]{:T(128)}) while((s32[]{:T(128)}, f32[512,512]{1,0:T(8,128)S(1)}, s32[4,2]{0,1:T(2,128)S(1)}, f32[4,128,128]{2,1,0:T(8,128)S(1)}, s32[]{:T(128)}) %tuple.44), condition=%wide.while_cond, body=%wide.while_body.sunk | while | flops 2 | bytes 131181 | solution.py:13
  26.3 1.3 bitcast_dynamic-update-slice_fusion.4
  28.3 1.3 bitcast_dynamic-update-slice_fusion.4
  30.2 1.3 bitcast_dynamic-update-slice_fusion.4
  32.1 1.3 bitcast_dynamic-update-slice_fusion.4
  33.4 39.3 %custom-call.4 = f32[4,128,128]{1,2,0:T(8,128)S(1)} custom-call(f32[4,128,128]{2,1,0:T(8,128)S(1)} %get-tuple-element.21), custom_call_target="InvertDiagBlocksLowerTriangular" | custom-call | tf_op jit(solution)/shard_map/triangular_solve/custom-call.1 | solution.py:13
  72.8 7.7 %while.5 = (s32[]{:T(128)}, f32[512,512]{1,0:T(8,128)S(1)}, s32[4,2]{0,1:T(2,128)S(1)}, f32[4,128,128]{2,1,0:T(8,128)S(1)}, s32[]{:T(128)}) while((s32[]{:T(128)}, f32[512,512]{1,0:T(8,128)S(1)}, s32[4,2]{0,1:T(2,128)S(1)}, f32[4,128,128]{2,1,0:T(8,128)S(1)}, s32[]{:T(128)}) %tuple.53), condition=%wide.while_cond.clone, body=%wide.while_body.clone.sunk | while | flops 2 | bytes 131181 | solution.py:13
  73.4 1.3 bitcast_dynamic-update-slice_fusion.5
  75.3 1.3 bitcast_dynamic-update-slice_fusion.5
  77.2 1.3 bitcast_dynamic-update-slice_fusion.5
  79.1 1.3 bitcast_dynamic-update-slice_fusion.5
  80.5 39.3 %custom-call.5 = f32[4,128,128]{1,2,0:T(8,128)S(1)} custom-call(f32[4,128,128]{2,1,0:T(8,128)S(1)} %get-tuple-element.22), custom_call_target="InvertDiagBlocksLowerTriangular" | custom-call | tf_op jit(solution)/shard_map/triangular_solve/custom-call.1 | solution.py:13
  119.9 4.2 %fusion.84 = (f32[1,2,512,512]{3,2,1,0:T(8,128)}, f32[1,2,512,512]{3,2,1,0:T(8,128)S(1)}) fusion(f32[2,2,512,512]{3,2,1,0:T(8,128)} %param.10), kind=kLoop, calls=%fused_computation.180 | loop fusion | bytes 8388608 | tf_op jit(solution)/shard_map/slice | solution.py:74
  124.1 4.1 %all-reduce.5.cloned.1.call-done = (f32[2048,128]{1,0:T(8,128)}, f32[512,512]{1,0:T(8,128)}) async-done(((f32[2048,128]{1,0:T(8,128)}, f32[512,512]{1,0:T(8,128)}), (f32[2048,128]{1,0:T(8,128)}, f32[512,512]{1,0:T(8,128)})) %all-reduce.5.cloned.1.call-update) | async-done | bytes 2097168 | tf_op jit(solution)/shard_map/psum | solution.py:53
  128.2 1.2 fusion.41
  129.4 1.1 convolution_subtract_fusion.4
  130.8 1.2 convolution_subtract_fusion.3
  132.3 1.2 convolution_subtract_fusion.6
  133.9 1.9 %convolution_subtract_fusion = f32[512,128]{1,0:T(8,128)S(1)} fusion(f32[512,512]{1,0:T(8,128)S(1)} %copy-done.3, f32[2048,128]{1,0:T(8,128)} %get-tuple-element.39, f32[128,128]{1,0:T(8,128)S(1)} %fusion.37, f32[128,128]{1,0:T(8,128)S(1)} %fusion.38, f32[128,128]{1,0:T(8,128)S(1)} %fusion.40, f32[128,128]{1,0:T(8,128)S(1)} %fusion.41), kind=kOutput, calls=%fused_computation.18 | convolution fusion | flops 402915328 | bytes 1835008 | tf_op jit(solution)/shard_map/dot_general | solution.py:19
  136.1 1.0 convolution_subtract_fusion.2
  137.4 1.2 convolution_subtract_fusion.1
  138.9 1.2 convolution_subtract_fusion.5
  140.5 3.9 %scatter_custom_fusion = f32[1024,128]{1,0:T(8,128)S(1)} fusion(f32[1024,128]{1,0:T(8,128)S(1)} %bitcast.92, s32[1024]{0:T(1024)S(1)} %bitcast.98, f32[2048,128]{1,0:T(8,128)} %get-tuple-element.39), kind=kCustom, calls=%fused_computation.34 | custom fusion | bytes 1048576 | tf_op jit(solution)/shard_map/scatter | solution.py:58
  144.4 3.7 %scatter_custom_fusion.1 = f32[1024,128]{1,0:T(8,128)S(1)} fusion(f32[1024,128]{1,0:T(8,128)S(1)} %scatter_custom_fusion, s32[1024]{0:T(1024)S(1)} %compare_select_fusion.3, f32[2048,128]{1,0:T(8,128)} %get-tuple-element.39), kind=kCustom, calls=%fused_computation.32 | custom fusion | bytes 1048576 | tf_op jit(solution)/shard_map/scatter | solution.py:60
  148.2 1.8 %fusion.1 = f32[1024,128]{1,0:T(8,128)S(1)} fusion(f32[1024,128]{1,0:T(8,128)S(1)} %scatter_custom_fusion.1, f32[1024,512]{1,0:T(8,128)S(1)} %bitcast.93, pred[1024]{0:T(1024)(128)(4,1)S(1)} %get-tuple-element.58, f32[128,128]{1,0:T(8,128)S(1)} %fusion.37, f32[128,128]{1,0:T(8,128)S(1)} %fusion.38, f32[128,128]{1,0:T(8,128)S(1)} %fusion.40, ...), kind=kOutput, calls=%fused_computation.13 | convolution fusion | flops 805765120 | bytes 3408896 | tf_op jit(solution)/shard_map/dot_general | solution.py:19
  150.0 3.0 %fusion.5 = f32[1024,128]{1,0:T(8,128)} fusion(f32[1024,128]{1,0:T(8,128)S(1)} %fusion.1, f32[512,128]{1,0:T(8,128)S(1)} %pad_maximum_fusion.2, f32[1024,512]{1,0:T(8,128)S(1)} %bitcast.94, f32[512,128]{1,0:T(8,128)S(1)} %pad_maximum_fusion.1, pred[1024]{0:T(1024)(128)(4,1)S(1)} %get-tuple-element.56, pred[1024]{0:T(1024)(128)(4,1)S(1)} %get-tuple-element.57, ...), kind=kOutput, calls=%fused_computation.17 | convolution fusion | flops 805830656 | bytes 3673088 | tf_op jit(solution)/shard_map/dot_general | solution.py:19
  (50 shorter events, 9.1 us)
Async XLA Ops:
  6.5 121.7 %all-reduce.5.cloned.1.call-start = ((), (), s32[]{:S(2)}) async-start(), calls=%async_computation | async-start | bytes 4194304 | tf_op jit(solution)/shard_map/psum | solution.py:53
  33.4 86.4 %copy-start.2 = (f32[512,512]{1,0:T(8,128)}, f32[512,512]{1,0:T(8,128)S(1)}, u32[]{:S(2)}) copy-start(f32[512,512]{1,0:T(8,128)S(1)} %get-tuple-element.155) | copy-start | bytes 3145732
  80.5 39.4 %copy-start.1 = (f32[512,512]{1,0:T(8,128)}, f32[512,512]{1,0:T(8,128)S(1)}, u32[]{:S(2)}) copy-start(f32[512,512]{1,0:T(8,128)S(1)} %get-tuple-element.154) | copy-start | bytes 3145732
  128.2 5.7 %copy-start.3 = (f32[512,512]{1,0:T(8,128)S(1)}, f32[512,512]{1,0:T(8,128)}, u32[]{:S(2)}) copy-start(f32[512,512]{1,0:T(8,128)} %get-tuple-element.40) | copy-start | bytes 3145732
  148.2 1.8 %copy-start = (f32[1,2,512,512]{3,2,1,0:T(8,128)S(1)}, f32[1,2,512,512]{3,2,1,0:T(8,128)}, u32[]{:S(2)}) copy-start(f32[1,2,512,512]{3,2,1,0:T(8,128)} %get-tuple-element.47) | copy-start | bytes 6291460
Sparse Core Ops, SparseCore 0:
  24.0 104.1 all-reduce.4
where the time goes:
time: 161 us; the launch traced here: 160 us
  other arithmetic  84.8 us (53%)
  local copies, waits for them, and re-layouts  33.8 us (21%)
  matrix products  16.9 us (10%)
  between operations  13.7 us (9%)
  blocking collectives  6.32 us (4%)
  waiting for transfers between devices  4.09 us (3%)
    another operation x7, other arithmetic, unit_lower_solve(): lax.linalg.triangular_solve(factor, values, left_side=True, lower=True, u...  80.4 us
    another operation x27, local copies, waits for them, and re-layouts, unit_lower_solve(): lax.linalg.triangular_solve(factor, values, left_side=True, lower=True, u...  15.2 us
    another operation x14, matrix products, unit_lower_solve(): lax.linalg.triangular_solve(factor, values, left_side=True, lower=True, u...  10.2 us
    scatter x2, local copies, waits for them, and re-layouts, shards(): permuted = flat.at[panel_landing].set(panel_moved, mode='drop').at[fresh_...  7.65 us
    dot_general x3, matrix products, product(): jnp.dot(left, right, precision=lax.Precision.HIGHEST, preferred_element_t...  6.77 us
    all_gather x1, blocking collectives, shards(): listed = lax.all_gather(pivots, 'cols', axis=0, tiled=True)  6.32 us
    gather x2, local copies, waits for them, and re-layouts, fetch(): return (jnp.take(flat, src_cycle * blk + src_row, axis=0), src_owner)  5.62 us
    slice x1, local copies, waits for them, and re-layouts, shards(): lower[1]  4.23 us
  transfers between devices with their start and end apart: 1, of which 1 were waited for; matrix products, arithmetic and copies ran while one was open for 62% of the time, Pallas kernels for 0%

commit v1 on v0

v1 whole, which is shorter than its diff:
```python
import functools

import jax
import jax.numpy as jnp
from jax import lax
from jax.experimental import pallas as pl
from jax.experimental.pallas import tpu as pltpu
from jax.sharding import PartitionSpec as P

MESH = pl.DeviceIdType.MESH
F32, BF16 = jnp.float32, jnp.bfloat16


def split(x):
    hi = x.astype(BF16)
    return hi, (x - hi.astype(F32)).astype(BF16)


def mm(a, b):
    return jnp.dot(a, b, preferred_element_type=F32)


def dot3(a, b):
    (ah, al), (bh, bl) = a, b
    return mm(ah, bh) + (mm(ah, bl) + mm(al, bh))


def wide(x):
    return jnp.concatenate(split(x), axis=1)


def fold(x):
    half = x.shape[1] // 2
    return x[:, :half] + x[:, half:]


def dot_wide(a, b):
    hi, lo = split(b)
    return fold(mm(a[0], jnp.concatenate([hi, lo], axis=1))) + mm(a[1], hi)


def select_rows(onehot, x):
    return fold(mm(onehot, wide(x)))


def iota(shape, dim):
    return lax.broadcasted_iota(jnp.int32, shape, dim)


def kernel(
    ranks, groups, blk, slots, chunks,
    rhs, diag_hbm, mult_hbm, piv, out,
    panels, lbuf, comp, pivs, diag, mult, inv, mhi, mlo,
    local_sem, piv_s, piv_r, pan_up, pan_ac, pan_r, l_up, l_ac, l_r, lc_s, lc_r,
    c_up, c_dn, c_ac, c_r,
):
    m, c = lax.axis_index("rows"), lax.axis_index("cols")
    steps = ranks // 2
    j, p = m // 2, m % 2
    local_count, columns = rhs.shape
    count = 2 * blk
    hb = blk // 2
    across = m + 1 - 2 * p
    has_up, has_dn = j < steps - 1, j > 0
    up = lax.rem(m + 2, ranks)
    dn = lax.rem(m + ranks - 2, ranks)
    pending = []

    copies = [
        pltpu.make_async_copy(mult_hbm.at[0], mult.at[0], local_sem.at[0]),
        pltpu.make_async_copy(diag_hbm, diag, local_sem.at[1]),
        pltpu.make_async_copy(mult_hbm.at[1], mult.at[1], local_sem.at[2]),
    ]
    for copy in copies:
        copy.start()

    barrier = pltpu.get_barrier_semaphore()

    def greet(**where):
        pl.semaphore_signal(barrier, inc=1, device_id=where, device_id_type=MESH)

    for d in range(1, groups):
        greet(cols=lax.rem(c + d, groups))
    greet(rows=across)

    @pl.when(has_up)
    def _():
        greet(rows=up)

    @pl.when(has_dn)
    def _():
        greet(rows=dn)

    met = groups + jnp.where(has_up, 1, 0) + jnp.where(has_dn, 1, 0)
    pl.semaphore_wait(barrier, met)

    def when(cond, action):
        if cond is None:
            action()
        else:
            pl.when(cond)(action)

    def remote(src, dst, ss, rs, **where):
        return pltpu.make_async_remote_copy(
            src_ref=src, dst_ref=dst, send_sem=ss, recv_sem=rs,
            device_id=where, device_id_type=MESH,
        )

    def send(cond, *args, **where):
        copy = remote(*args, **where)
        when(cond, copy.start)
        pending.append((cond, copy))

    for d in range(1, groups):
        send(None, piv, pivs.at[c], piv_s.at[d - 1], piv_r.at[c], cols=lax.rem(c + d, groups))

    rows_per = blk // chunks

    def chunk(q):
        return pl.ds(q * rows_per, rows_per)

    for q in range(chunks):
        dst = panels.at[p, chunk(q)]
        sem = pan_r.at[p * chunks + q]
        send(j == 0, rhs.at[chunk(q)], dst, pan_up.at[q], sem, rows=up)
        send(j == 0, rhs.at[chunk(q)], dst, pan_ac.at[q], sem, rows=across)

    qr = blk // groups
    hr = qr // 2

    def lpart(h):
        return pl.ds(pl.multiple_of(c * qr + h * hr, 8), hr)

    copies[0].wait()
    send(m == 1, mult.at[0, lpart(0)], lbuf.at[lpart(0)], l_up.at[0], l_r.at[0], rows=up)
    for h in (1, 0):
        send(m == 1, mult.at[0, lpart(h)], lbuf.at[lpart(h)], l_ac.at[h], l_r.at[h], rows=across)

    @pl.when(j == 0)
    def _():
        panels[p] = rhs[:blk]

    @pl.when(m == 1)
    def _():
        lbuf[...] = mult[0, :blk]

    pivs[c] = piv[...]
    copies[1].wait()

    r_at, c_at = iota((hb, hb), 0), iota((hb, hb), 1)

    def offdiag(b, k, h):
        pair = (r_at // (2 * b) == c_at // (2 * b)) & (r_at % (2 * b) >= b) & (c_at % (2 * b) < b)
        return jnp.where(pair, diag[k, h * hb:(h + 1) * hb, h * hb:(h + 1) * hb], 0.0)

    def level(b):
        for k in range(2):
            for h in range(2):
                at = 2 * k + h
                f = offdiag(b, k, h)
                if b == 1:
                    inv[at] = jnp.where(r_at == c_at, 1.0, 0.0) - f
                else:
                    x = inv[at]
                    xs = split(x)
                    inv[at] = x - dot3(split(dot3(xs, split(f))), xs)

    def levels(lo, hi):
        b = lo
        while b < hi:
            level(b)
            b *= 2

    for d in range(1, groups):
        src = lax.rem(c + d, groups)
        remote(piv, pivs.at[src], piv_s.at[d - 1], piv_r.at[src], cols=src).wait_recv()
    pr = piv.shape[0]
    listed = pivs[...].reshape(groups * pr, 128)
    shift = blk.bit_length() - 1
    rshift = ranks.bit_length() - 1
    fresh = listed >= count
    owner = jnp.where(fresh, (listed >> shift) & (ranks - 1), -1)
    place = ((listed >> (shift + rshift)) << shift) | (listed & (blk - 1))
    ownf, placef = owner.astype(F32), place.astype(F32)

    def column(x):
        xt = x.T
        return jnp.concatenate([xt[:, k:k + 1] for k in range(groups * pr)], axis=0)

    def flat_row(x):
        return jnp.concatenate([x[k:k + 1] for k in range(groups * pr)], axis=1)

    own_col, place_col = column(ownf), column(placef)
    lanes = -(-ranks // 128) * 128
    own_hot = own_col == iota((count, lanes), 1).astype(F32)
    before = (iota((count, count), 0) > iota((count, count), 1)).astype(F32).astype(BF16)
    tally = mm(before, own_hot.astype(F32).astype(BF16))
    slot_col = jnp.sum(jnp.where(own_hot, tally, 0.0), axis=1, keepdims=True)
    mf = m.astype(F32)
    wide_slots = -(-slots // 128) * 128
    taken = (slot_col == iota((count, wide_slots), 1).astype(F32)) & (own_col == mf)
    src_row = jnp.sum(jnp.where(taken, place_col + 1.0, 0.0), axis=0, keepdims=True) - 1.0
    src_col = jnp.broadcast_to(src_row, (8, wide_slots)).T[:slots, :1]
    pick = (src_col == iota((slots, local_count), 1).astype(F32)).astype(F32).astype(BF16)

    def slab(r):
        return pl.ds(pl.multiple_of(r * slots, 8), slots)

    comp[slab(m)] = select_rows(pick, rhs[...])

    def pass_on(r, go_up, go_dn, go_ac):
        for cond, sem, to in ((go_up, c_up, up), (go_dn, c_dn, dn), (go_ac, c_ac, across)):
            if cond is not False:
                send(cond, comp.at[slab(r)], comp.at[slab(r)], sem.at[r], c_r.at[r], rows=to)

    def arrived(cond, dst, sem):
        when(cond, remote(dst, dst, l_up.at[0], sem, rows=across).wait_recv)

    pass_on(m, has_up, has_dn, None)
    levels(1, 4)

    for q in range(chunks):
        here = panels.at[p, chunk(q)]
        sem = pan_r.at[p * chunks + q]
        arrived(has_dn, here, sem)
        send(has_dn & has_up, here, here, pan_up.at[q], sem, rows=up)
        send(has_dn, here, here, pan_ac.at[q], sem, rows=across)
    mine_half = 1 - p
    here = lbuf.at[lpart(mine_half)]
    arrived(m != 1, here, l_r.at[mine_half])
    send((m != 1) & has_up, here, here, l_up.at[0], l_r.at[mine_half], rows=up)
    send(has_dn, here, here, l_ac.at[mine_half], l_r.at[mine_half], rows=across)

    def share(h):
        for d in range(1, groups):
            to = lax.rem(c + d, groups)
            part = lbuf.at[lpart(h)]
            send(m != 1, part, part, lc_s.at[h * (groups - 1) + d - 1], lc_r.at[c * 2 + h], cols=to)

    share(mine_half)

    span = hb // 4
    b = 4
    for s in range(1, steps):
        below, above = lax.rem(m - 2 * s + ranks, ranks), lax.rem(m + 2 * s, ranks)
        from_below, from_above = j >= s, j + s < steps
        arrived(from_below, comp.at[slab(below)], c_r.at[below])
        pass_on(below, from_below & has_up, False, from_below)
        arrived(from_above, comp.at[slab(above)], c_r.at[above])
        pass_on(above, False, from_above & has_dn, from_above)
        if b < hb:
            levels(b, b * 4 if s < steps - 1 else hb)
            b = b * 4
    levels(b, hb)

    other_half = p
    arrived(m != 1, lbuf.at[lpart(other_half)], l_r.at[other_half])
    share(other_half)

    copies[2].wait()
    mhi[...], mlo[...] = split(mult[...])

    for q in range(chunks):
        arrived(None, panels.at[1 - p, chunk(q)], pan_r.at[(1 - p) * chunks + q])

    to_here = jnp.where(owner == m, place, -1).astype(F32)
    to_row = flat_row(to_here)
    landing = (iota((local_count, count), 0).astype(F32) == to_row).astype(F32)
    hit = jnp.sum(landing, axis=1, keepdims=True) > 0.0
    moved_in = select_rows(landing.astype(BF16), panels[...].reshape(count, columns))
    out[...] = jnp.where(hit, moved_in, rhs[...])

    for s in range(steps):
        r = 2 * s + 1 - p
        arrived(None, comp.at[slab(r)], c_r.at[r])

    where_col = jnp.where(own_col >= 0.0, own_col * slots + slot_col, -1.0)
    pool = wide(comp[...])

    def panel_rows(k):
        target = where_col[k * blk:(k + 1) * blk]
        pick = (target == iota((blk, ranks * slots), 1).astype(F32)).astype(F32).astype(BF16)
        return jnp.where(target >= 0.0, fold(mm(pick, pool)), panels[k])

    def solve(k, values):
        first = dot_wide(split(inv[2 * k]), values[:hb])
        rest = values[hb:] - dot_wide(split(diag[k, hb:, :hb]), first)
        return jnp.concatenate([first, dot_wide(split(inv[2 * k + 1]), rest)], axis=0)

    y0 = solve(0, panel_rows(0))
    start = panel_rows(1)

    def gather_lower(h):
        for d in range(1, groups):
            src = lax.rem(c + d, groups)
            part = lbuf.at[pl.ds(pl.multiple_of(src * qr + h * hr, 8), hr)]
            arrived(m != 1, part, lc_r.at[src * 2 + h])

    gather_lower(0)
    gather_lower(1)
    y1 = solve(1, start - dot_wide(split(lbuf[...]), y0))
    out[...] = out[...] - dot_wide((mhi[0], mlo[0]), y0) - dot_wide((mhi[1], mlo[1]), y1)

    @pl.when(m == 0)
    def _():
        out[:blk] = y0

    @pl.when(m == 1)
    def _():
        out[:blk] = y1

    for cond, copy in pending:
        when(cond, copy.wait_send)


def shards(ranks, groups, rhs, diag_blocks, multipliers, pivots):
    cycles, blk, columns = rhs.shape
    local_count = cycles * blk
    count = pivots.shape[0] * groups
    slots = 3 * count // (2 * ranks)
    chunks = 4
    dma = pltpu.SemaphoreType.DMA
    solved = pl.pallas_call(
        functools.partial(kernel, ranks, groups, blk, slots, chunks),
        out_shape=jax.ShapeDtypeStruct((local_count, columns), F32),
        in_specs=[
            pl.BlockSpec(memory_space=pltpu.VMEM),
            pl.BlockSpec(memory_space=pl.ANY),
            pl.BlockSpec(memory_space=pl.ANY),
            pl.BlockSpec(memory_space=pltpu.VMEM),
        ],
        out_specs=pl.BlockSpec(memory_space=pltpu.VMEM),
        scratch_shapes=[
            pltpu.VMEM((2, blk, columns), F32),
            pltpu.VMEM((blk, blk), F32),
            pltpu.VMEM((ranks * slots, columns), F32),
            pltpu.VMEM((groups, pivots.shape[0] // 128, 128), jnp.int32),
            pltpu.VMEM((2, blk, blk), F32),
            pltpu.VMEM((2, local_count, blk), F32),
            pltpu.VMEM((4, blk // 2, blk // 2), F32),
            pltpu.VMEM((2, local_count, blk), BF16),
            pltpu.VMEM((2, local_count, blk), BF16),
            dma((3,)), dma((groups,)), dma((groups,)),
            dma((chunks,)), dma((chunks,)), dma((2 * chunks,)),
            dma((1,)), dma((2,)), dma((2,)),
            dma((2 * groups,)), dma((2 * groups,)),
            dma((ranks,)), dma((ranks,)), dma((ranks,)), dma((ranks,)),
        ],
        compiler_params=pltpu.CompilerParams(
            collective_id=0, has_side_effects=True, vmem_limit_bytes=60 * 1024 * 1024
        ),
    )(
        rhs.reshape(local_count, columns),
        diag_blocks,
        multipliers.reshape(multipliers.shape[0], local_count, blk),
        pivots.reshape(-1, 128),
    )
    return solved.reshape(cycles, blk, columns)


def solution(mesh):
    placed = (P(None, "rows", "cols"), P(), P(None, None, "rows", None), P("cols"))
    return jax.shard_map(
        functools.partial(shards, mesh.shape["rows"], mesh.shape["cols"]),
        mesh=mesh, in_specs=placed, out_specs=P(None, "rows", "cols"), check_vma=False,
    )
```

time: 161 us -> 44.2 us (0.27)
  other arithmetic: 84.8 us -> 0 us
  Pallas kernels: 0 us -> 41.6 us
  local copies, waits for them, and re-layouts: 33.8 us -> 1.87 us
  matrix products: 16.9 us -> 0 us
  between operations: 13.7 us -> 0.01 us
  blocking collectives: 6.32 us -> 0 us
  waiting for transfers between devices: 4.09 us -> 0 us
    another operation x7 -> x0, other arithmetic: 80.4 us -> none  [unit_lower_solve(): lax.linalg.triangular_solve(factor, values, left_side=True, lower=True, u...]
    pallas_call x0 -> x1, Pallas kernels: none -> 41.6 us  [shards(): pl.pallas_call(functools.partial(kernel, ranks, groups, blk, slots, chunk...]
    another operation x27 -> x0, local copies, waits for them, and re-layouts: 15.2 us -> none  [unit_lower_solve(): lax.linalg.triangular_solve(factor, values, left_side=True, lower=True, u...]
    another operation x14 -> x0, matrix products: 10.2 us -> none  [unit_lower_solve(): lax.linalg.triangular_solve(factor, values, left_side=True, lower=True, u...]
    scatter x2 -> x0, local copies, waits for them, and re-layouts: 7.65 us -> none  [shards(): permuted = flat.at[panel_landing].set(panel_moved, mode='drop').at[fresh_...]
    dot_general x3 -> x0, matrix products: 6.77 us -> none  [product(): jnp.dot(left, right, precision=lax.Precision.HIGHEST, preferred_element_t...]
    all_gather x1 -> x0, blocking collectives: 6.32 us -> none  [shards(): listed = lax.all_gather(pivots, 'cols', axis=0, tiled=True)]
    gather x2 -> x0, local copies, waits for them, and re-layouts: 5.62 us -> none  [fetch(): return (jnp.take(flat, src_cycle * blk + src_row, axis=0), src_owner)]
  transfers between devices with their start and end apart: 1 -> 0, of which waited for: 1 -> 0; matrix products, arithmetic and copies ran while one was open for 62% -> 0% of each run, Pallas kernels for 0% -> 0%
where the time goes in v1:
time: 44.2 us; the launch traced here: 43.5 us
  Pallas kernels  41.6 us (94%)
  local copies, waits for them, and re-layouts  1.87 us (4%)
    pallas_call x1, Pallas kernels, shards(): pl.pallas_call(functools.partial(kernel, ranks, groups, blk, slots, chunk...  41.6 us
    unnamed x1, local copies, waits for them, and re-layouts  1.87 us

profile of v1, /device:TPU:0, one launch (start us, length us, event | category | flops | bytes accessed | tf_op | source)
XLA Modules:
  0.0 43.5 jit_solution(4197024031666407247)
XLA Ops:
  0.0 41.6 %shard_map.46 = f32[1024,128]{1,0:T(8,128)} custom-call(f32[1024,128]{1,0:T(8,128)} %bitcast.6, f32[2,512,512]{2,1,0:T(8,128)} %diag_hbm.1, f32[2,1024,512]{2,1,0:T(8,128)} %bitcast.4, s32[2,128]{1,0:T(2,128)} %bitcast.7), custom_call_target="tpu_custom_call" | custom-call | tf_op jit(solution)/shard_map/pallas_call | solution.py:323
  41.6 1.9 %copy.6 = f32[2,512,128]{2,1,0:T(8,128)} copy(f32[2,512,128]{2,1,0:T(8,128)} %bitcast.5) | data formatting | bytes 1048576

commit v2 on v1

--- a/solution.py
+++ b/solution.py
@@ -48,10 +48,10 @@
 
 
 def kernel(
-    ranks, groups, blk, slots, chunks,
+    ranks, groups, blk, slots, chunks, parts,
     rhs, diag_hbm, mult_hbm, piv, out,
     panels, lbuf, comp, pivs, diag, mult, inv, mhi, mlo,
-    local_sem, piv_s, piv_r, pan_up, pan_ac, pan_r, l_up, l_ac, l_r, lc_s, lc_r,
+    local_sem, piv_s, piv_r, pan_up, pan_ac, pan_r, l_up, l_ac, l_r, lc_s, lc_f, lc_r,
     c_up, c_dn, c_ac, c_r,
 ):
     m, c = lax.axis_index("rows"), lax.axis_index("cols")
@@ -119,22 +119,31 @@
     def chunk(q):
         return pl.ds(q * rows_per, rows_per)
 
-    for q in range(chunks):
+    qr = blk // groups
+    hr = qr // 2 // chunks
+
+    def lpart(h, q, owner=c):
+        return lbuf.at[pl.ds(pl.multiple_of(owner * qr + (h * chunks + q) * hr, 8), hr)]
+
+    def lsource(h, q):
+        return mult.at[0, pl.ds(pl.multiple_of(c * qr + (h * chunks + q) * hr, 8), hr)]
+
+    def lsem(h, q):
+        return l_r.at[h * chunks + q]
+
+    def panel_source(q):
         dst = panels.at[p, chunk(q)]
         sem = pan_r.at[p * chunks + q]
         send(j == 0, rhs.at[chunk(q)], dst, pan_up.at[q], sem, rows=up)
         send(j == 0, rhs.at[chunk(q)], dst, pan_ac.at[q], sem, rows=across)
 
-    qr = blk // groups
-    hr = qr // 2
-
-    def lpart(h):
-        return pl.ds(pl.multiple_of(c * qr + h * hr, 8), hr)
-
     copies[0].wait()
-    send(m == 1, mult.at[0, lpart(0)], lbuf.at[lpart(0)], l_up.at[0], l_r.at[0], rows=up)
-    for h in (1, 0):
-        send(m == 1, mult.at[0, lpart(h)], lbuf.at[lpart(h)], l_ac.at[h], l_r.at[h], rows=across)
+    for q in range(chunks):
+        send(m == 1, lsource(1, q), lpart(1, q), l_ac.at[chunks + q], lsem(1, q), rows=across)
+    for q in range(chunks):
+        send(m == 1, lsource(0, q), lpart(0, q), l_up.at[q], lsem(0, q), rows=up)
+        send(m == 1, lsource(0, q), lpart(0, q), l_ac.at[q], lsem(0, q), rows=across)
+        panel_source(q)
 
     @pl.when(j == 0)
     def _():
@@ -171,6 +180,33 @@
             level(b)
             b *= 2
 
+    mine_half = 1 - p
+    side = c + 1 - 2 * (c % 2)
+    far = lax.rem(c + 2, groups)
+    corner = groups - 1 - c
+
+    def share(h, q, cond):
+        part, at = lpart(h, q), h * chunks + q
+        for n, to in enumerate((far, side)):
+            send(cond, part, part, lc_s.at[n * 2 * chunks + at], lc_r.at[c * 2 * chunks + at], cols=to)
+
+    def relay(q, cond):
+        here = lpart(mine_half, q)
+        arrived(cond & (m != 1), here, lsem(mine_half, q))
+        send(cond & (m != 1) & has_up, here, here, l_up.at[q], lsem(mine_half, q), rows=up)
+        send(cond & has_dn, here, here, l_ac.at[mine_half * chunks + q], lsem(mine_half, q), rows=across)
+        share(mine_half, q, cond & (m != 1))
+        here = panels.at[p, chunk(q)]
+        sem = pan_r.at[p * chunks + q]
+        arrived(cond & has_dn, here, sem)
+        send(cond & has_dn & has_up, here, here, pan_up.at[q], sem, rows=up)
+        send(cond & has_dn, here, here, pan_ac.at[q], sem, rows=across)
+
+    def arrived(cond, dst, sem):
+        when(cond, remote(dst, dst, l_up.at[0], sem, rows=across).wait_recv)
+
+    early = j <= 1
+
     for d in range(1, groups):
         src = lax.rem(c + d, groups)
         remote(piv, pivs.at[src], piv_s.at[d - 1], piv_r.at[src], cols=src).wait_recv()
@@ -190,6 +226,7 @@
     def flat_row(x):
         return jnp.concatenate([x[k:k + 1] for k in range(groups * pr)], axis=1)
 
+    relay(0, early)
     own_col, place_col = column(ownf), column(placef)
     lanes = -(-ranks // 128) * 128
     own_hot = own_col == iota((count, lanes), 1).astype(F32)
@@ -206,56 +243,48 @@
     def slab(r):
         return pl.ds(pl.multiple_of(r * slots, 8), slots)
 
+    part_rows = slots // parts
+
+    def slice_of(r, n):
+        return comp.at[pl.ds(pl.multiple_of(r * slots + n * part_rows, 8), part_rows)]
+
     comp[slab(m)] = select_rows(pick, rhs[...])
 
-    def pass_on(r, go_up, go_dn, go_ac):
+    def pass_on(r, n, go_up, go_dn, go_ac):
+        here, at = slice_of(r, n), r * parts + n
         for cond, sem, to in ((go_up, c_up, up), (go_dn, c_dn, dn), (go_ac, c_ac, across)):
             if cond is not False:
-                send(cond, comp.at[slab(r)], comp.at[slab(r)], sem.at[r], c_r.at[r], rows=to)
-
-    def arrived(cond, dst, sem):
-        when(cond, remote(dst, dst, l_up.at[0], sem, rows=across).wait_recv)
-
-    pass_on(m, has_up, has_dn, None)
+                send(cond, here, here, sem.at[at], c_r.at[at], rows=to)
+
+    for n in range(parts):
+        pass_on(m, n, has_up, has_dn, None)
+
+    relay(0, jnp.logical_not(early))
     levels(1, 4)
 
-    for q in range(chunks):
-        here = panels.at[p, chunk(q)]
-        sem = pan_r.at[p * chunks + q]
-        arrived(has_dn, here, sem)
-        send(has_dn & has_up, here, here, pan_up.at[q], sem, rows=up)
-        send(has_dn, here, here, pan_ac.at[q], sem, rows=across)
-    mine_half = 1 - p
-    here = lbuf.at[lpart(mine_half)]
-    arrived(m != 1, here, l_r.at[mine_half])
-    send((m != 1) & has_up, here, here, l_up.at[0], l_r.at[mine_half], rows=up)
-    send(has_dn, here, here, l_ac.at[mine_half], l_r.at[mine_half], rows=across)
-
-    def share(h):
-        for d in range(1, groups):
-            to = lax.rem(c + d, groups)
-            part = lbuf.at[lpart(h)]
-            send(m != 1, part, part, lc_s.at[h * (groups - 1) + d - 1], lc_r.at[c * 2 + h], cols=to)
-
-    share(mine_half)
-
-    span = hb // 4
     b = 4
+    ready = 1
     for s in range(1, steps):
+        for q in range(ready, min(ready + 2, chunks)):
+            relay(q, j >= 0)
+        ready = min(ready + 2, chunks)
         below, above = lax.rem(m - 2 * s + ranks, ranks), lax.rem(m + 2 * s, ranks)
         from_below, from_above = j >= s, j + s < steps
-        arrived(from_below, comp.at[slab(below)], c_r.at[below])
-        pass_on(below, from_below & has_up, False, from_below)
-        arrived(from_above, comp.at[slab(above)], c_r.at[above])
-        pass_on(above, False, from_above & has_dn, from_above)
+        for n in range(parts):
+            arrived(from_above, slice_of(above, n), c_r.at[above * parts + n])
+            pass_on(above, n, False, from_above & has_dn, from_above)
+        for n in range(parts):
+            arrived(from_below, slice_of(below, n), c_r.at[below * parts + n])
+            pass_on(below, n, from_below & has_up, False, from_below)
         if b < hb:
             levels(b, b * 4 if s < steps - 1 else hb)
             b = b * 4
     levels(b, hb)
 
     other_half = p
-    arrived(m != 1, lbuf.at[lpart(other_half)], l_r.at[other_half])
-    share(other_half)
+    for q in range(chunks):
+        arrived(m != 1, lpart(other_half, q), lsem(other_half, q))
+        share(other_half, q, m != 1)
 
     copies[2].wait()
     mhi[...], mlo[...] = split(mult[...])
@@ -270,9 +299,19 @@
     moved_in = select_rows(landing.astype(BF16), panels[...].reshape(count, columns))
     out[...] = jnp.where(hit, moved_in, rhs[...])
 
+    def forward(h):
+        for q in range(chunks):
+            part, at = lpart(h, q, far), h * chunks + q
+            sem = lc_r.at[far * 2 * chunks + at]
+            arrived(m != 1, part, sem)
+            send(m != 1, part, part, lc_f.at[at], sem, cols=side)
+
+    forward(0)
+    forward(1)
     for s in range(steps):
         r = 2 * s + 1 - p
-        arrived(None, comp.at[slab(r)], c_r.at[r])
+        for n in range(parts):
+            arrived(None, slice_of(r, n), c_r.at[r * parts + n])
 
     where_col = jnp.where(own_col >= 0.0, own_col * slots + slot_col, -1.0)
     pool = wide(comp[...])
@@ -290,14 +329,10 @@
     y0 = solve(0, panel_rows(0))
     start = panel_rows(1)
 
-    def gather_lower(h):
-        for d in range(1, groups):
-            src = lax.rem(c + d, groups)
-            part = lbuf.at[pl.ds(pl.multiple_of(src * qr + h * hr, 8), hr)]
-            arrived(m != 1, part, lc_r.at[src * 2 + h])
-
-    gather_lower(0)
-    gather_lower(1)
+    for owner in (side, corner):
+        for h in range(2):
+            for q in range(chunks):
+                arrived(m != 1, lpart(h, q, owner), lc_r.at[(owner * 2 + h) * chunks + q])
     y1 = solve(1, start - dot_wide(split(lbuf[...]), y0))
     out[...] = out[...] - dot_wide((mhi[0], mlo[0]), y0) - dot_wide((mhi[1], mlo[1]), y1)
 
@@ -318,10 +353,10 @@
     local_count = cycles * blk
     count = pivots.shape[0] * groups
     slots = 3 * count // (2 * ranks)
-    chunks = 4
+    chunks, parts = 4, 3
     dma = pltpu.SemaphoreType.DMA
     solved = pl.pallas_call(
-        functools.partial(kernel, ranks, groups, blk, slots, chunks),
+        functools.partial(kernel, ranks, groups, blk, slots, chunks, parts),
         out_shape=jax.ShapeDtypeStruct((local_count, columns), F32),
         in_specs=[
             pl.BlockSpec(memory_space=pltpu.VMEM),
@@ -342,9 +377,9 @@
             pltpu.VMEM((2, local_count, blk), BF16),
             dma((3,)), dma((groups,)), dma((groups,)),
             dma((chunks,)), dma((chunks,)), dma((2 * chunks,)),
-            dma((1,)), dma((2,)), dma((2,)),
-            dma((2 * groups,)), dma((2 * groups,)),
-            dma((ranks,)), dma((ranks,)), dma((ranks,)), dma((ranks,)),
+            dma((chunks,)), dma((2 * chunks,)), dma((2 * chunks,)),
+            dma((4 * chunks,)), dma((2 * chunks,)), dma((2 * groups * chunks,)),
+            dma((ranks * parts,)), dma((ranks * parts,)), dma((ranks * parts,)), dma((ranks * parts,)),
         ],
         compiler_params=pltpu.CompilerParams(
             collective_id=0, has_side_effects=True, vmem_limit_bytes=60 * 1024 * 1024

time: 44.2 us -> 47.6 us (1.077); the launches traced: 43.5 us -> 47.5 us
  Pallas kernels: 41.6 us -> 45.6 us
    pallas_call x1, Pallas kernels: 41.6 us -> 45.6 us  [shards(): pl.pallas_call(functools.partial(kernel, ranks, groups, blk, slots, chunk...]
where the time goes in v2:
time: 47.6 us; the launch traced here: 47.5 us
  Pallas kernels  45.6 us (96%)
  local copies, waits for them, and re-layouts  1.87 us (4%)
    pallas_call x1, Pallas kernels, shards(): pl.pallas_call(functools.partial(kernel, ranks, groups, blk, slots, chunk...  45.6 us
    unnamed x1, local copies, waits for them, and re-layouts  1.87 us

profile of v2, /device:TPU:0, one launch (start us, length us, event | category | flops | bytes accessed | tf_op | source)
XLA Modules:
  0.0 47.5 jit_solution(1108904905931715079)
XLA Ops:
  0.0 45.6 %shard_map.46 = f32[1024,128]{1,0:T(8,128)} custom-call(f32[1024,128]{1,0:T(8,128)} %bitcast.6, f32[2,512,512]{2,1,0:T(8,128)} %diag_hbm.1, f32[2,1024,512]{2,1,0:T(8,128)} %bitcast.4, s32[2,128]{1,0:T(2,128)} %bitcast.7), custom_call_target="tpu_custom_call" | custom-call | tf_op jit(solution)/shard_map/pallas_call | solution.py:358
  45.6 1.9 %copy.6 = f32[2,512,128]{2,1,0:T(8,128)} copy(f32[2,512,128]{2,1,0:T(8,128)} %bitcast.5) | data formatting | bytes 1048576
